TPU v7x, 32 devices: a whole 2x2x4 slice. The times are simulated.
32 devices in a mesh: rows: 4 (over z), cx: 2 (over y), cy: 4 (over x, core).
Axes of the slice: x: 2, y: 2, z: 4, core: 2. Of those that a mesh axis runs over, the one named last changes fastest.
Arguments:
- rows_data: float32 [2048, 1024], P(('rows', 'cx', 'cy')), may hold values from -6 to 6
- owner_rows: int32 [2048, 1], P(('rows', 'cx', 'cy')), may hold values from 0 to 7; in each aligned block of 64 rows (0 to 63, 64 to 127, ...) at most 16 rows name the same one
- slot_rows: int32 [2048], P(('rows', 'cx', 'cy')), may hold values from 0 to 2047
- centroids: float32 [16384, 1024], P(('cx', 'cy'), 'rows'), may hold values from -6 to 6
- counts: float32 [16384], P(('cx', 'cy')), may hold values from 1 to 100
- owner_cent: int32 [16384, 1], P(('cx', 'cy')), may hold values from 0 to 7; in each aligned block of 2048 rows (0 to 2047, 2048 to 4095, ...) at most 512 rows name the same one
- slot_cent: int32 [16384], P(('cx', 'cy')), may hold values from 0 to 511
- upper: float32 [4096, 1024], P(('cx', 'cy'), 'rows'), may hold values from -6 to 6
- upper_counts: float32 [4096], P(('cx', 'cy')), may hold values from 1 to 100
Outputs:
- moved: float32 [16384, 1024], P(('cx', 'cy'), 'rows')
- new_counts: float32 [16384], P(('cx', 'cy'))
- new_upper: float32 [4096, 1024], P(('cx', 'cy'), 'rows')
- new_upper_counts: float32 [4096], P(('cx', 'cy'))
Inputs may be any that keep to these rules, and one draw needn't show every extreme that they name: `owner_rows`: the rows of one device name each value at most 16 times, and some device reaches it. `owner_cent`: the 2048 level-1 centroids of one shard name each value at most 512 times, and some shard reaches it.
All inputs are finite; a program needn't handle non-finite values.
Results may differ from a plain program's by a relative error of at most 0.00002.
Values sent between devices are 32-bit elements; how exact they have to be, the bound alone decides.
A program may use at most 64 MiB of HBM per device.

v0:
```python
import jax
import jax.numpy as jnp
from jax import lax
from jax.sharding import PartitionSpec as P


def bucket(values, owners, slot_ids, shards, capacity, empty):
    onehot = (owners[:, None] == jnp.arange(shards, dtype=jnp.int32)[None, :]).astype(jnp.int32)
    earlier = jnp.cumsum(onehot, axis=0) - onehot
    position = jnp.sum(earlier * onehot, axis=1)
    target = owners * capacity + position
    buffer = jnp.zeros((shards * capacity, values.shape[1]), values.dtype).at[target].set(values)
    labels = jnp.full((shards * capacity,), empty, jnp.int32).at[target].set(slot_ids)
    return (buffer.reshape(shards, capacity, values.shape[1]), labels.reshape(shards, capacity))


def accumulate(values, labels, segments):
    summed = jnp.zeros((segments, values.shape[1]), jnp.float32).at[labels].add(values, mode="drop")
    member_counts = (
        jnp.zeros((segments,), jnp.float32)
        .at[labels]
        .add(jnp.ones(labels.shape, jnp.float32), mode="drop")
    )
    return (summed, member_counts)


def damped(previous, weights, summed, member_counts):
    denominator = weights + member_counts
    updated = previous + (summed - member_counts[:, None] * previous) / denominator[:, None]
    return (updated, denominator)


def body(
    rows_data, owner_rows, slot_rows, centroids, counts, owner_cent, slot_cent, upper, upper_counts
):
    shards = lax.axis_size(("cx", "cy"))
    groups = lax.axis_size("rows")
    batch = rows_data.shape[0]
    lower_rows = centroids.shape[0]
    capacity = 2 * batch // shards
    buffer, labels = bucket(rows_data, owner_rows[:, 0], slot_rows, shards, capacity, lower_rows)
    labels = jnp.broadcast_to(labels[:, :, None], (shards, capacity, groups))
    arrived, arrived_labels = (
        lax.all_to_all(
            lax.all_to_all(buffer, "rows", split_axis=2, concat_axis=1, tiled=True),
            ("cx", "cy"),
            split_axis=0,
            concat_axis=0,
            tiled=True,
        ),
        lax.all_to_all(
            lax.all_to_all(labels, "rows", split_axis=2, concat_axis=1, tiled=True),
            ("cx", "cy"),
            split_axis=0,
            concat_axis=0,
            tiled=True,
        ),
    )
    slice_width = arrived.shape[2]
    summed, member_counts = accumulate(
        arrived.reshape(-1, slice_width), arrived_labels.reshape(-1), lower_rows
    )
    moved, new_counts = damped(centroids, counts, summed, member_counts)
    upper_rows = upper.shape[0]
    owners_upper = owner_cent[:, 0]
    labels_upper = owners_upper * upper_rows + slot_cent
    whole_partial, hit_counts = accumulate(moved, labels_upper, upper_rows * shards)
    upper_summed = lax.psum_scatter(whole_partial, ("cx", "cy"), scatter_dimension=0, tiled=True)
    upper_members = lax.psum_scatter(hit_counts, ("cx", "cy"), scatter_dimension=0, tiled=True)
    new_upper, new_upper_counts = damped(upper, upper_counts, upper_summed, upper_members)
    return (moved, new_counts, new_upper, new_upper_counts)


def solution(mesh):
    placed = (
        P(("rows", "cx", "cy"), None),
        P(("rows", "cx", "cy"), None),
        P(("rows", "cx", "cy")),
        P(("cx", "cy"), "rows"),
        P(("cx", "cy")),
        P(("cx", "cy"), None),
        P(("cx", "cy")),
        P(("cx", "cy"), "rows"),
        P(("cx", "cy")),
    )
    return jax.shard_map(
        body,
        mesh=mesh,
        in_specs=placed,
        out_specs=(
            P(("cx", "cy"), "rows"),
            P(("cx", "cy")),
            P(("cx", "cy"), "rows"),
            P(("cx", "cy")),
        ),
        check_vma=False,
    )
```

profile of v0, /device:TPU:0, one launch (start us, length us, event | category | flops | bytes accessed | tf_op | source)
XLA Modules:
  0.0 151.4 jit_solution(6357609695715163591)
XLA Ops:
  7.2 0.7 fusion.6
  8.0 0.8 select_reduce_fusion
  9.5 0.9 scatter_custom_fusion
  11.2 6.3 %all-to-all-start = ((s32[4,1,128]{2,1,0:T(1,128)}), s32[4,1,128]{2,1,0:T(1,128)S(1)}, u32[]{:S(2)}, u32[]{:S(2)}) async-start(s32[4,1,128]{2,1,0:T(1,128)} %reshape.128), calls=%async_computation | async-start | bytes 4096 | tf_op jit(solution)/shard_map/all_to_all | solution.py:52
  17.5 1.4 scatter_custom_fusion.1
  18.9 2.6 %copy.16 = f32[8,16,1024]{1,0,2:T(8,128)} copy(f32[8,16,1024]{2,1,0:T(8,128)S(1)} %bitcast.33) | data formatting | bytes 1048576 | tf_op jit(solution)/shard_map/reshape | solution.py:14
  21.5 4.6 %reshape.130 = f32[4,1,32768]{2,1,0:T(1,128)} reshape(f32[1024,8,16]{2,1,0:T(8,128)} %bitcast.31) | data formatting | bytes 1048576
  26.1 5.1 %all-to-all-start.2 = ((f32[4,1,32768]{2,1,0:T(1,128)}), f32[4,1,32768]{2,1,0:T(1,128)S(1)}, u32[]{:S(2)}, u32[]{:S(2)}) async-start(f32[4,1,32768]{2,1,0:T(1,128)} %reshape.130), calls=%async_computation.2 | async-start | bytes 1048576 | tf_op jit(solution)/shard_map/all_to_all | solution.py:45
  33.1 12.0 %all-to-all-done.2 = f32[4,1,32768]{2,1,0:T(1,128)S(1)} async-done(((f32[4,1,32768]{2,1,0:T(1,128)}), f32[4,1,32768]{2,1,0:T(1,128)S(1)}, u32[]{:S(2)}, u32[]{:S(2)}) %all-to-all-start.2) | async-done | bytes 524320 | tf_op jit(solution)/shard_map/all_to_all | solution.py:45
  45.1 3.7 %all-to-all-start.1 = ((s32[8,64,1]{1,2,0:T(1,128)}), s32[8,64,1]{1,2,0:T(1,128)S(1)}, u32[]{:S(2)}, u32[]{:S(2)}) async-start(s32[8,64,1]{1,2,0:T(1,128)} %bitcast.5), calls=%async_computation.1 | async-start | bytes 8192 | tf_op jit(solution)/shard_map/all_to_all | solution.py:51
  49.3 2.1 %reduce.5 = f32[4,32768]{1,0:T(4,128)S(1)} reduce(f32[4,1,32768]{2,1,0:T(1,128)S(1)} %all-to-all-done.2, f32[]{:T(128)} %broadcast.65), dimensions={1}, to_apply=%all_to_all.37.reduce_sub_computation | reduce | bytes 1048580 | tf_op jit(solution)/shard_map/all_to_all | solution.py:45
  51.5 3.4 %reshape.131 = f32[1024,8,16]{2,1,0:T(8,128)} reshape(f32[4,32768]{1,0:T(4,128)S(1)} %reduce.5) | data formatting | bytes 1048576
  54.9 2.8 %copy.19 = f32[8,16,4,256]{3,2,1,0:T(4,128)S(1)} copy(f32[8,16,4,256]{1,0,3,2:T(8,128)} %bitcast.32) | data formatting | bytes 1048576 | tf_op jit(solution)/shard_map/all_to_all | solution.py:45
  57.8 0.9 copy.18
  58.7 4.2 %all-to-all-start.3 = ((f32[8,64,256]{2,1,0:T(8,128)}), f32[8,64,256]{2,1,0:T(8,128)S(1)}, u32[]{:S(2)}, u32[]{:S(2)}) async-start(f32[8,64,256]{2,1,0:T(8,128)} %bitcast.10), calls=%async_computation.3 | async-start | bytes 1048576 | tf_op jit(solution)/shard_map/all_to_all | solution.py:44
  64.2 3.2 %scatter_custom_fusion.3 = f32[2048]{0:T(1024)S(1)} fusion(s32[512]{0:T(512)S(1)} %bitcast.39, f32[512]{0:T(512)S(1)} %broadcast.51, f32[]{:T(128)} %constant.8.clone.1), kind=kCustom, calls=%fused_computation.22 | custom fusion | flops 512 | bytes 8196 | tf_op jit(solution)/shard_map/scatter-add | solution.py:22
  67.5 5.1 %all-to-all-done.3 = f32[8,64,256]{2,1,0:T(8,128)S(1)} async-done(((f32[8,64,256]{2,1,0:T(8,128)}), f32[8,64,256]{2,1,0:T(8,128)S(1)}, u32[]{:S(2)}, u32[]{:S(2)}) %all-to-all-start.3) | async-done | bytes 524320 | tf_op jit(solution)/shard_map/all_to_all | solution.py:44
  72.6 4.0 %scatter_custom_fusion.2 = f32[2048,256]{1,0:T(8,128)S(1)} fusion(s32[512]{0:T(512)S(1)} %bitcast.40, f32[512,256]{1,0:T(8,128)S(1)} %bitcast.35, f32[]{:T(128)} %constant.8.clone.1), kind=kCustom, calls=%fused_computation.9 | custom fusion | flops 131072 | bytes 2097156 | tf_op jit(solution)/shard_map/scatter-add | solution.py:18
  76.6 2.9 %divide_add_fusion = f32[2048,256]{1,0:T(8,128)} fusion(f32[2048,256]{1,0:T(8,128)} %param.12, f32[2048,256]{1,0:T(8,128)S(1)} %scatter_custom_fusion.2, f32[2048]{0:T(1024)S(1)} %add.54, f32[2048]{0:T(1024)S(1)} %scatter_custom_fusion.3), kind=kLoop, calls=%fused_computation.8 | loop fusion | flops 2097152 | bytes 6307840 | tf_op jit(solution)/shard_map/add | solution.py:29
  79.5 14.1 %scatter_custom_fusion.4 = f32[4096,256]{1,0:T(8,128)} fusion(s32[2048]{0:T(1024)S(1)} %compare_select_fusion, f32[2048,256]{1,0:T(8,128)} %divide_add_fusion, f32[]{:T(128)} %constant.8.clone.1), kind=kCustom, calls=%fused_computation.6 | custom fusion | flops 524288 | bytes 4194816 | tf_op jit(solution)/shard_map/scatter-add | solution.py:18
  93.6 11.2 %scatter_custom_fusion.5 = f32[4096]{0:T(1024)S(1)} fusion(s32[2048]{0:T(1024)S(1)} %compare_select_fusion, f32[2048]{0:T(1024)S(1)} %broadcast.52, f32[]{:T(128)} %constant.8.clone.1), kind=kCustom, calls=%fused_computation.19 | custom fusion | flops 2048 | bytes 16388 | tf_op jit(solution)/shard_map/scatter-add | solution.py:22
  106.2 23.2 %all-reduce = f32[4096]{0:T(1024)S(1)} all-reduce(f32[4096]{0:T(1024)S(1)} %scatter_custom_fusion.5), channel_id=3, replica_groups=mesh['rows'=4,'cx'=2,'cy'=4] {'cx','cy'}, use_global_device_ids=true, to_apply=%region_9.10.clone | all-reduce | flops 4096 | bytes 32768
  129.4 13.1 %reduce-scatter.2.cloned.1.call-done = f32[512,256]{1,0:T(8,128)} async-done(((f32[4096,256]{1,0:T(8,128)}), f32[512,256]{1,0:T(8,128)}) %reduce-scatter.2.cloned.1.call-update) | async-done | bytes 524304 | tf_op jit(solution)/shard_map/reduce_scatter | solution.py:68
  142.5 2.0 %divide_add_fusion.1 = f32[512,256]{1,0:T(8,128)} fusion(f32[512,256]{1,0:T(8,128)S(1)} %copy-done, f32[512,256]{1,0:T(8,128)} %reduce-scatter.2.cloned.1.call-done, f32[512]{0:T(512)S(1)} %get-tuple-element.4, f32[512]{0:T(512)S(1)} %get-tuple-element.5), kind=kLoop, calls=%fused_computation.11 | loop fusion | flops 524288 | bytes 1576960 | tf_op jit(solution)/shard_map/add | solution.py:29
  (43 shorter events, 6.0 us)
Async XLA Ops:
  11.2 14.9 %all-to-all-start = ((s32[4,1,128]{2,1,0:T(1,128)}), s32[4,1,128]{2,1,0:T(1,128)S(1)}, u32[]{:S(2)}, u32[]{:S(2)}) async-start(s32[4,1,128]{2,1,0:T(1,128)} %reshape.128), calls=%async_computation | async-start | bytes 4096 | tf_op jit(solution)/shard_map/all_to_all | solution.py:52
  26.1 19.0 %all-to-all-start.2 = ((f32[4,1,32768]{2,1,0:T(1,128)}), f32[4,1,32768]{2,1,0:T(1,128)S(1)}, u32[]{:S(2)}, u32[]{:S(2)}) async-start(f32[4,1,32768]{2,1,0:T(1,128)} %reshape.130), calls=%async_computation.2 | async-start | bytes 1048576 | tf_op jit(solution)/shard_map/all_to_all | solution.py:45
  45.1 13.5 %all-to-all-start.1 = ((s32[8,64,1]{1,2,0:T(1,128)}), s32[8,64,1]{1,2,0:T(1,128)S(1)}, u32[]{:S(2)}, u32[]{:S(2)}) async-start(s32[8,64,1]{1,2,0:T(1,128)} %bitcast.5), calls=%async_computation.1 | async-start | bytes 8192 | tf_op jit(solution)/shard_map/all_to_all | solution.py:51
  57.7 5.2 %copy-start.5 = (s32[2048,1]{0,1:T(1,128)S(1)}, s32[2048,1]{0,1:T(1,128)}, u32[]{:S(2)}) copy-start(s32[2048,1]{0,1:T(1,128)} %param.14) | copy-start | bytes 24580
  57.7 5.2 %copy-start.3 = (s32[2048]{0:T(1024)S(1)}, s32[2048]{0:T(1024)}, u32[]{:S(2)}) copy-start(s32[2048]{0:T(1024)} %param.15) | copy-start | bytes 24580
  57.8 9.7 %copy-start.4 = (f32[2048]{0:T(1024)S(1)}, f32[2048]{0:T(1024)}, u32[]{:S(2)}) copy-start(f32[2048]{0:T(1024)} %param.13) | copy-start | bytes 24580
  58.7 13.9 %all-to-all-start.3 = ((f32[8,64,256]{2,1,0:T(8,128)}), f32[8,64,256]{2,1,0:T(8,128)S(1)}, u32[]{:S(2)}, u32[]{:S(2)}) async-start(f32[8,64,256]{2,1,0:T(8,128)} %bitcast.10), calls=%async_computation.3 | async-start | bytes 1048576 | tf_op jit(solution)/shard_map/all_to_all | solution.py:44
  62.9 79.6 %reduce-scatter.2.cloned.1.call-start = ((), (), s32[]{:S(2)}) async-start(), calls=%async_computation.5 | async-start | bytes 4718592 | tf_op jit(solution)/shard_map/reduce_scatter | solution.py:68
  67.5 12.0 %copy-start.1 = (f32[2048]{0:T(1024)}, f32[2048]{0:T(1024)S(1)}, u32[]{:S(2)}) copy-start(f32[2048]{0:T(1024)S(1)} %add.54) | copy-start | bytes 24580
  93.6 11.3 %copy-start.7 = (u32[32]{0:T(128)S(1)}, u32[32]{0:T(128)}, u32[]{:S(2)}) copy-start(u32[32]{0:T(128)} %constant.5) | copy-start | bytes 388
  93.6 35.7 %copy-start.6 = (f32[512]{0:T(512)S(1)}, f32[512]{0:T(512)}, u32[]{:S(2)}) copy-start(f32[512]{0:T(512)} %param.17) | copy-start | bytes 6148
  93.6 48.9 %copy-start = (f32[512,256]{1,0:T(8,128)S(1)}, f32[512,256]{1,0:T(8,128)}, u32[]{:S(2)}) copy-start(f32[512,256]{1,0:T(8,128)} %param.16) | copy-start | bytes 1572868
  129.4 15.1 %copy-start.2 = (f32[512]{0:T(512)}, f32[512]{0:T(512)S(1)}, u32[]{:S(2)}) copy-start(f32[512]{0:T(512)S(1)} %get-tuple-element.4) | copy-start | bytes 6148
Sparse Core Ops, SparseCore 0:
  93.8 48.6 reduce-scatter.1
where the time goes:
time: 152 us; the launch traced here: 151 us
  other arithmetic  43.4 us (29%)
  waiting for transfers between devices  30.1 us (20%)
  blocking collectives  23.2 us (15%)
  local copies, waits for them, and re-layouts  20.4 us (13%)
  starting transfers between devices  19.4 us (13%)
  between operations  14.9 us (10%)
    unnamed x1, blocking collectives  23.2 us
    scatter-add x2, other arithmetic, accumulate(): jnp.zeros((segments, values.shape[1]), jnp.float32).at[labels]  18.1 us
    scatter-add x2, other arithmetic, accumulate(): member_counts = jnp.zeros((segments,), jnp.float32).at[labels].add(jnp.on...  14.5 us
    reduce_scatter x1, waiting for transfers between devices, body(): lax.psum_scatter(whole_partial, ('cx', 'cy'), scatter_dimension=0, tiled=...  13.1 us
    all_to_all x1, waiting for transfers between devices, body(): lax.all_to_all(buffer, 'rows', split_axis=2, concat_axis=1, tiled=True)  12 us
    unnamed x22, local copies, waits for them, and re-layouts  9.38 us
    all_to_all x1, starting transfers between devices, body(): lax.all_to_all(labels, 'rows', split_axis=2, concat_axis=1, tiled=True)  6.35 us
    all_to_all x1, starting transfers between devices, body(): lax.all_to_all(buffer, 'rows', split_axis=2, concat_axis=1, tiled=True)  5.09 us
  transfers between devices with their start and end apart: 5, of which 3 were waited for; matrix products, arithmetic and copies ran while one was open for 24% of the time, Pallas kernels for 0%

commit v1 on v0

--- a/solution.py
+++ b/solution.py
@@ -2,6 +2,13 @@
 import jax.numpy as jnp
 from jax import lax
 from jax.sharding import PartitionSpec as P
+
+
+def trade_parts(shard, mesh_axis, split, join):
+    n_dev = lax.axis_size(mesh_axis)
+    shards = jnp.stack(jnp.split(shard, n_dev, axis=split), axis=0)
+    shards = lax.all_to_all(shards, mesh_axis, split_axis=0, concat_axis=0)
+    return jnp.concatenate(shards, axis=join)
 
 
 def bucket(values, owners, slot_ids, shards, capacity, empty):
@@ -42,11 +49,7 @@
     labels = jnp.broadcast_to(labels[:, :, None], (shards, capacity, groups))
     arrived, arrived_labels = (
         lax.all_to_all(
-            lax.all_to_all(buffer, "rows", split_axis=2, concat_axis=1, tiled=True),
-            ("cx", "cy"),
-            split_axis=0,
-            concat_axis=0,
-            tiled=True,
+            trade_parts(buffer, "rows", 2, 1), ("cx", "cy"), split_axis=0, concat_axis=0, tiled=True
         ),
         lax.all_to_all(
             lax.all_to_all(labels, "rows", split_axis=2, concat_axis=1, tiled=True),

time: 152 us -> 140 us (0.921)
  local copies, waits for them, and re-layouts: 20.4 us -> 6.4 us
  waiting for transfers between devices: 30.1 us -> 36.4 us
  starting transfers between devices: 19.4 us -> 17.1 us
    unnamed x22 -> x20, local copies, waits for them, and re-layouts: 9.38 us -> 1.38 us
    all_to_all x1, waiting for transfers between devices: 0.01 us -> 3.78 us  [body(): lax.all_to_all(lax.all_to_all(labels, 'rows', split_axis=2, concat_axis=1...]
    all_to_all x3 -> x1, local copies, waits for them, and re-layouts: 4.24 us -> 0.84 us  [trade_parts(): shards = lax.all_to_all(shards, mesh_axis, split_axis=0, concat_axis=0)]
    all_to_all x1, waiting for transfers between devices: 0.01 us -> 3.21 us  [body(): lax.all_to_all(labels, 'rows', split_axis=2, concat_axis=1, tiled=True)]
    reshape x1 -> x0, local copies, waits for them, and re-layouts: 2.61 us -> none  [bucket(): buffer.reshape(shards, capacity, values.shape[1])]
    all_to_all x2, starting transfers between devices: 9.29 us -> 6.97 us  [the longest x1 3.49 us: body(): lax.all_to_all(trade_parts(buffer, 'rows', 2, 1), ('cx', 'cy'), split_axi...]
    all_to_all x1 -> x0, other arithmetic: 2.14 us -> none  [body(): lax.all_to_all(buffer, 'rows', split_axis=2, concat_axis=1, tiled=True)]
  transfers between devices with their start and end apart: 5 -> 5, of which waited for: 3 -> 5; matrix products, arithmetic and copies ran while one was open for 24% -> 15% of each run, Pallas kernels for 0% -> 0%
where the time goes in v1:
time: 140 us
  other arithmetic  42 us (30%)
  waiting for transfers between devices  36.4 us (26%)
  blocking collectives  23.2 us (17%)
  starting transfers between devices  17.1 us (12%)
  between operations  14.9 us (11%)
  local copies, waits for them, and re-layouts  6.4 us (5%)
    unnamed x1, blocking collectives  23.2 us
    scatter-add x2, other arithmetic, accumulate(): jnp.zeros((segments, values.shape[1]), jnp.float32).at[labels]  17.9 us
    scatter-add x2, other arithmetic, accumulate(): member_counts = jnp.zeros((segments,), jnp.float32).at[labels].add(jnp.on...  14.5 us
    reduce_scatter x1, waiting for transfers between devices, body(): lax.psum_scatter(whole_partial, ('cx', 'cy'), scatter_dimension=0, tiled=...  13.1 us
    all_to_all x1, waiting for transfers between devices, trade_parts(): shards = lax.all_to_all(shards, mesh_axis, split_axis=0, concat_axis=0)  11.4 us
    all_to_all x1, starting transfers between devices, body(): lax.all_to_all(labels, 'rows', split_axis=2, concat_axis=1, tiled=True)  6.35 us
    all_to_all x1, waiting for transfers between devices, body(): lax.all_to_all(trade_parts(buffer, 'rows', 2, 1), ('cx', 'cy'), split_axi...  5 us
    add x2, other arithmetic, damped(): previous + (summed - member_counts[:, None] * previous) / denominator[:,...  4.95 us
  transfers between devices with their start and end apart: 5, of which 5 were waited for; matrix products, arithmetic and copies ran while one was open for 15% of the time, Pallas kernels for 0%

profile of v1, /device:TPU:0, one launch (start us, length us, event | category | flops | bytes accessed | tf_op | source)
XLA Modules:
  0.0 139.9 jit_solution(7597728511747641311)
XLA Ops:
  7.2 0.7 fusion.6
  8.0 0.8 select_reduce_fusion
  8.8 0.7 fusion.11
  9.5 0.9 scatter_custom_fusion
  11.2 6.3 %all-to-all-start = ((s32[4,1,128]{2,1,0:T(1,128)}), s32[4,1,128]{2,1,0:T(1,128)S(1)}, u32[]{:S(2)}, u32[]{:S(2)}) async-start(s32[4,1,128]{2,1,0:T(1,128)} %reshape.136), calls=%async_computation | async-start | bytes 4096 | tf_op jit(solution)/shard_map/all_to_all | solution.py:55
  17.5 1.4 scatter_custom_fusion.1
  19.0 0.8 pad_maximum_fusion
  19.8 3.2 %all-to-all-done = s32[4,1,128]{2,1,0:T(1,128)S(1)} async-done(((s32[4,1,128]{2,1,0:T(1,128)}), s32[4,1,128]{2,1,0:T(1,128)S(1)}, u32[]{:S(2)}, u32[]{:S(2)}) %all-to-all-start) | async-done | bytes 2080 | tf_op jit(solution)/shard_map/all_to_all | solution.py:55
  23.0 3.5 %all-to-all-start.2 = ((f32[4,8,16,256]{3,2,1,0:T(8,128)}), f32[4,8,16,256]{3,2,1,0:T(8,128)S(1)}, u32[]{:S(2)}, u32[]{:S(2)}) async-start(f32[4,8,16,256]{3,2,1,0:T(8,128)} %pad_maximum_fusion), calls=%async_computation.2 | async-start | bytes 1048576 | tf_op jit(solution)/shard_map/all_to_all | solution.py:10
  27.8 0.7 all_to_all.25
  28.4 11.4 %all-to-all-done.2 = f32[4,8,16,256]{3,2,1,0:T(8,128)S(1)} async-done(((f32[4,8,16,256]{3,2,1,0:T(8,128)}), f32[4,8,16,256]{3,2,1,0:T(8,128)S(1)}, u32[]{:S(2)}, u32[]{:S(2)}) %all-to-all-start.2) | async-done | bytes 524320 | tf_op jit(solution)/shard_map/all_to_all | solution.py:10
  39.8 3.7 %all-to-all-start.1 = ((s32[8,64,1]{1,2,0:T(1,128)}), s32[8,64,1]{1,2,0:T(1,128)S(1)}, u32[]{:S(2)}, u32[]{:S(2)}) async-start(s32[8,64,1]{1,2,0:T(1,128)} %bitcast.5), calls=%async_computation.1 | async-start | bytes 8192 | tf_op jit(solution)/shard_map/all_to_all | solution.py:54
  43.5 0.8 copy.21
  44.4 3.8 %all-to-all-done.1 = s32[8,64,1]{1,2,0:T(1,128)S(1)} async-done(((s32[8,64,1]{1,2,0:T(1,128)}), s32[8,64,1]{1,2,0:T(1,128)S(1)}, u32[]{:S(2)}, u32[]{:S(2)}) %all-to-all-start.1) | async-done | bytes 2080 | tf_op jit(solution)/shard_map/all_to_all | solution.py:54
  48.1 3.5 %all-to-all-start.3 = ((f32[8,64,256]{2,1,0:T(8,128)}), f32[8,64,256]{2,1,0:T(8,128)S(1)}, u32[]{:S(2)}, u32[]{:S(2)}) async-start(f32[8,64,256]{2,1,0:T(8,128)} %bitcast.13), calls=%async_computation.3 | async-start | bytes 1048576 | tf_op jit(solution)/shard_map/all_to_all | solution.py:51
  53.0 3.2 %scatter_custom_fusion.3 = f32[2048]{0:T(1024)S(1)} fusion(s32[512]{0:T(512)S(1)} %bitcast.42, f32[512]{0:T(512)S(1)} %broadcast.51, f32[]{:T(128)} %constant.8.clone.1), kind=kCustom, calls=%fused_computation.27 | custom fusion | flops 512 | bytes 8196 | tf_op jit(solution)/shard_map/scatter-add | solution.py:29
  56.3 5.0 %all-to-all-done.3 = f32[8,64,256]{2,1,0:T(8,128)S(1)} async-done(((f32[8,64,256]{2,1,0:T(8,128)}), f32[8,64,256]{2,1,0:T(8,128)S(1)}, u32[]{:S(2)}, u32[]{:S(2)}) %all-to-all-start.3) | async-done | bytes 524320 | tf_op jit(solution)/shard_map/all_to_all | solution.py:51
  61.3 3.8 %scatter_custom_fusion.2 = f32[2048,256]{1,0:T(8,128)S(1)} fusion(s32[512]{0:T(512)S(1)} %bitcast.43, f32[512,256]{1,0:T(8,128)S(1)} %bitcast.38, f32[]{:T(128)} %constant.8.clone.1), kind=kCustom, calls=%fused_computation.9 | custom fusion | flops 131072 | bytes 2097156 | tf_op jit(solution)/shard_map/scatter-add | solution.py:25
  65.1 2.9 %divide_add_fusion = f32[2048,256]{1,0:T(8,128)} fusion(f32[2048,256]{1,0:T(8,128)} %param.12, f32[2048,256]{1,0:T(8,128)S(1)} %scatter_custom_fusion.2, f32[2048]{0:T(1024)S(1)} %add.54, f32[2048]{0:T(1024)S(1)} %scatter_custom_fusion.3), kind=kLoop, calls=%fused_computation.8 | loop fusion | flops 2097152 | bytes 6307840 | tf_op jit(solution)/shard_map/add | solution.py:36
  68.0 14.1 %scatter_custom_fusion.4 = f32[4096,256]{1,0:T(8,128)} fusion(s32[2048]{0:T(1024)S(1)} %compare_select_fusion, f32[2048,256]{1,0:T(8,128)} %divide_add_fusion, f32[]{:T(128)} %constant.8.clone.1), kind=kCustom, calls=%fused_computation.6 | custom fusion | flops 524288 | bytes 4194816 | tf_op jit(solution)/shard_map/scatter-add | solution.py:25
  82.2 11.2 %scatter_custom_fusion.5 = f32[4096]{0:T(1024)S(1)} fusion(s32[2048]{0:T(1024)S(1)} %compare_select_fusion, f32[2048]{0:T(1024)S(1)} %broadcast.52, f32[]{:T(128)} %constant.8.clone.1), kind=kCustom, calls=%fused_computation.24 | custom fusion | flops 2048 | bytes 16388 | tf_op jit(solution)/shard_map/scatter-add | solution.py:29
  94.7 23.2 %all-reduce = f32[4096]{0:T(1024)S(1)} all-reduce(f32[4096]{0:T(1024)S(1)} %scatter_custom_fusion.5), channel_id=3, replica_groups=mesh['rows'=4,'cx'=2,'cy'=4] {'cx','cy'}, use_global_device_ids=true, to_apply=%region_9.10.clone | all-reduce | flops 4096 | bytes 32768
  117.9 13.1 %reduce-scatter.2.cloned.1.call-done = f32[512,256]{1,0:T(8,128)} async-done(((f32[4096,256]{1,0:T(8,128)}), f32[512,256]{1,0:T(8,128)}) %reduce-scatter.2.cloned.1.call-update) | async-done | bytes 524304 | tf_op jit(solution)/shard_map/reduce_scatter | solution.py:71
  131.0 2.0 %divide_add_fusion.1 = f32[512,256]{1,0:T(8,128)} fusion(f32[512,256]{1,0:T(8,128)S(1)} %copy-done, f32[512,256]{1,0:T(8,128)} %reduce-scatter.2.cloned.1.call-done, f32[512]{0:T(512)S(1)} %get-tuple-element.4, f32[512]{0:T(512)S(1)} %get-tuple-element.5), kind=kLoop, calls=%fused_computation.12 | loop fusion | flops 524288 | bytes 1576960 | tf_op jit(solution)/shard_map/add | solution.py:36
  (39 shorter events, 4.2 us)
Async XLA Ops:
  11.2 11.8 %all-to-all-start = ((s32[4,1,128]{2,1,0:T(1,128)}), s32[4,1,128]{2,1,0:T(1,128)S(1)}, u32[]{:S(2)}, u32[]{:S(2)}) async-start(s32[4,1,128]{2,1,0:T(1,128)} %reshape.136), calls=%async_computation | async-start | bytes 4096 | tf_op jit(solution)/shard_map/all_to_all | solution.py:55
  18.9 32.8 %copy-start.5 = (s32[2048,1]{0,1:T(1,128)S(1)}, s32[2048,1]{0,1:T(1,128)}, u32[]{:S(2)}) copy-start(s32[2048,1]{0,1:T(1,128)} %param.14) | copy-start | bytes 24580
  18.9 32.8 %copy-start.3 = (s32[2048]{0:T(1024)S(1)}, s32[2048]{0:T(1024)}, u32[]{:S(2)}) copy-start(s32[2048]{0:T(1024)} %param.15) | copy-start | bytes 24580
  19.0 37.3 %copy-start.4 = (f32[2048]{0:T(1024)S(1)}, f32[2048]{0:T(1024)}, u32[]{:S(2)}) copy-start(f32[2048]{0:T(1024)} %param.13) | copy-start | bytes 24580
  23.0 16.8 %all-to-all-start.2 = ((f32[4,8,16,256]{3,2,1,0:T(8,128)}), f32[4,8,16,256]{3,2,1,0:T(8,128)S(1)}, u32[]{:S(2)}, u32[]{:S(2)}) async-start(f32[4,8,16,256]{3,2,1,0:T(8,128)} %pad_maximum_fusion), calls=%async_computation.2 | async-start | bytes 1048576 | tf_op jit(solution)/shard_map/all_to_all | solution.py:10
  39.8 8.3 %all-to-all-start.1 = ((s32[8,64,1]{1,2,0:T(1,128)}), s32[8,64,1]{1,2,0:T(1,128)S(1)}, u32[]{:S(2)}, u32[]{:S(2)}) async-start(s32[8,64,1]{1,2,0:T(1,128)} %bitcast.5), calls=%async_computation.1 | async-start | bytes 8192 | tf_op jit(solution)/shard_map/all_to_all | solution.py:54
  48.1 13.2 %all-to-all-start.3 = ((f32[8,64,256]{2,1,0:T(8,128)}), f32[8,64,256]{2,1,0:T(8,128)S(1)}, u32[]{:S(2)}, u32[]{:S(2)}) async-start(f32[8,64,256]{2,1,0:T(8,128)} %bitcast.13), calls=%async_computation.3 | async-start | bytes 1048576 | tf_op jit(solution)/shard_map/all_to_all | solution.py:51
  51.6 79.4 %reduce-scatter.2.cloned.1.call-start = ((), (), s32[]{:S(2)}) async-start(), calls=%async_computation.5 | async-start | bytes 4718592 | tf_op jit(solution)/shard_map/reduce_scatter | solution.py:71
  56.3 11.7 %copy-start.1 = (f32[2048]{0:T(1024)}, f32[2048]{0:T(1024)S(1)}, u32[]{:S(2)}) copy-start(f32[2048]{0:T(1024)S(1)} %add.54) | copy-start | bytes 24580
  82.1 11.3 %copy-start.7 = (u32[32]{0:T(128)S(1)}, u32[32]{0:T(128)}, u32[]{:S(2)}) copy-start(u32[32]{0:T(128)} %constant.5) | copy-start | bytes 388
  82.1 35.7 %copy-start.6 = (f32[512]{0:T(512)S(1)}, f32[512]{0:T(512)}, u32[]{:S(2)}) copy-start(f32[512]{0:T(512)} %param.17) | copy-start | bytes 6148
  82.1 48.9 %copy-start = (f32[512,256]{1,0:T(8,128)S(1)}, f32[512,256]{1,0:T(8,128)}, u32[]{:S(2)}) copy-start(f32[512,256]{1,0:T(8,128)} %param.16) | copy-start | bytes 1572868
  117.9 15.1 %copy-start.2 = (f32[512]{0:T(512)}, f32[512]{0:T(512)S(1)}, u32[]{:S(2)}) copy-start(f32[512]{0:T(512)S(1)} %get-tuple-element.4) | copy-start | bytes 6148
Sparse Core Ops, SparseCore 0:
  82.3 48.6 reduce-scatter.1
